TPU v7x, 128 devices: a whole 4x4x4 slice. The times are simulated.
128 devices in a mesh: isl: 4 (over z_hi, core), fsdp: 32 (over x, z_lo, y).
Axes of the slice: x: 4, y: 4, z: 4 (z_hi: 2, z_lo: 2; z = z_hi * 2 + z_lo), core: 2. Of those that a mesh axis runs over, the one named last changes fastest.
Arguments:
- weights: float32 [3, 7168, 4096], P(None, 'fsdp', 'isl'), may hold values from -6 to 6
- momentum: float32 [3, 7168, 4096], P(None, 'fsdp', 'isl'), may hold values from -0.12 to 0.12
- first_moment: bfloat16 [4, 3, 7168, 4096], P('isl', None, 'fsdp'), may hold values from -0.00029945374 to 0.00029945374
- second_moment: bfloat16 [4, 3, 7168, 4096], P('isl', None, 'fsdp'), may hold values from 9.95351e-09 to 9.953976e-06
- inputs: bfloat16 [2, 1024, 4096], P(None, ('isl', 'fsdp')), may hold values from -6 to 6
- targets: bfloat16 [2, 1024, 4096], P(None, ('isl', 'fsdp')), may hold values from -6 to 6
- overflow_step: int32 [4, 32], P('isl', 'fsdp'), may hold values from 0 to 63
Outputs:
- new_weights: float32 [3, 7168, 4096], P(None, 'fsdp', 'isl')
- new_momentum: float32 [3, 7168, 4096], P(None, 'fsdp', 'isl')
Inputs may be any that keep to these rules, and one draw needn't show every extreme that they name: `overflow_step`: A device reports an overflow at inner step k when its value equals k; values of 2 or more report none.
All inputs are finite; a program needn't handle non-finite values.
Results may differ from a plain program's by a relative error of at most 0.004.
Values may be sent and summed in bfloat16 or wider, within the bound.
No kernel may reach another device: no remote copies, remote signals or barrier semaphores. Data moves between devices by JAX's collectives and lax.ppermute only.
A program may use at most 128 MiB of HBM per device.

v0:
```python
import math
import jax
import jax.numpy as jnp
from jax import lax
from jax.sharding import PartitionSpec as P

D = 4096
FF = 7168
inner_rate = 0.02
beta_first = 0.9
beta_second = 0.95
epsilon = 1e-08
decay_rate = 0.1
outer_rate = 0.7
nesterov_coef = 0.9


def joined_along(parts, dim):
    dims = list(parts.shape[1:])
    dims[dim] *= parts.shape[0]
    return jnp.moveaxis(parts, 0, dim).reshape(dims)


def copy_for_each(shard, axis):
    copies = jnp.broadcast_to(shard, (lax.axis_size(axis), *shard.shape))
    return lax.all_to_all(copies, axis, split_axis=0, concat_axis=0, tiled=True)


def collect(shard, axis, dim):
    return joined_along(copy_for_each(shard, axis), dim)


def taken_together(shard, axis):
    return copy_for_each(shard, axis).sum(axis=0)


def split_up(shard, dim, devices):
    before, after = (shard.shape[:dim], shard.shape[dim + 1 :])
    return jnp.moveaxis(shard.reshape(*before, devices, -1, *after), dim, 0)


def sum_at_owner(shard, axis, dim):
    devices = lax.axis_size(axis)
    parts = lax.all_to_all(split_up(shard, dim, devices), axis, 0, 0, tiled=True)
    return jnp.sum(parts, axis=0)


def silu_parts(preact):
    sigmoid_value = jax.nn.sigmoid(preact)
    return (preact * sigmoid_value, sigmoid_value * (1.0 + preact * (1.0 - sigmoid_value)))


def contract_last(left_side, right_side):
    return lax.dot_general(
        left_side, right_side, (((1,), (1,)), ((), ())), preferred_element_type=jnp.float32
    )


def contract_first(left_side, right_side):
    return lax.dot_general(
        left_side, right_side, (((0,), (0,)), ((), ())), preferred_element_type=jnp.float32
    )


def body(weights, momentum, first_moment, second_moment, inputs, targets, overflow_step):
    island_count = lax.axis_size("isl")
    gathered = collect(weights.astype(jnp.bfloat16), "isl", 2).astype(weights.dtype)
    current = gathered
    moment_one = first_moment[0].astype(jnp.float32)
    moment_two = second_moment[0].astype(jnp.float32)
    inner_count = inputs.shape[0]
    island_tokens = inputs.shape[1] * lax.axis_size("fsdp")
    overflow_marks = (overflow_step.reshape(1) == jnp.arange(inner_count, dtype=jnp.int32)).astype(
        jnp.int32
    )
    overflow_counts = taken_together(overflow_marks, "fsdp")
    all_inputs = lax.all_gather(inputs, "fsdp", axis=1, tiled=True)
    for inner_step in range(inner_count):
        rounded = current.astype(jnp.bfloat16)
        local_inputs = inputs[inner_step]
        local_targets = targets[inner_step]
        every_input = all_inputs[inner_step]
        gate_pre = contract_last(every_input, rounded[0]) / math.sqrt(D)
        up_pre = contract_last(every_input, rounded[1]) / math.sqrt(D)
        activated, slope = silu_parts(gate_pre)
        hidden = (activated * up_pre).astype(jnp.bfloat16)
        partial_value = jnp.dot(hidden, rounded[2], preferred_element_type=jnp.float32)
        summed = sum_at_owner(partial_value, "fsdp", 0)
        outputs = local_inputs.astype(jnp.float32) + summed / math.sqrt(FF)
        own_slopes = ((outputs - local_targets.astype(jnp.float32)) / island_tokens).astype(
            jnp.bfloat16
        )
        slopes = collect(own_slopes, "fsdp", 0)
        hidden_slope = contract_last(slopes, rounded[2]) / math.sqrt(FF)
        gate_slope = (hidden_slope * up_pre * slope).astype(jnp.bfloat16)
        up_slope = (hidden_slope * activated).astype(jnp.bfloat16)
        grad_gate = contract_first(gate_slope, every_input) / math.sqrt(D)
        grad_up = contract_first(up_slope, every_input) / math.sqrt(D)
        grad_down = contract_first(hidden, slopes) / math.sqrt(FF)
        gradient = jnp.stack([grad_gate, grad_up, grad_down])
        overflow_count = overflow_counts[inner_step]
        skipped = overflow_count > 0
        next_one = beta_first * moment_one + (1.0 - beta_first) * gradient
        next_two = beta_second * moment_two + (1.0 - beta_second) * gradient * gradient
        next_weights = current - inner_rate * (
            next_one / (jnp.sqrt(next_two) + epsilon) + decay_rate * current
        )
        current = jnp.where(skipped, current, next_weights)
        moment_one = jnp.where(skipped, moment_one, next_one)
        moment_two = jnp.where(skipped, moment_two, next_two)
    pseudo_term = gathered - current
    pseudo_sum = lax.psum_scatter(
        pseudo_term.astype(jnp.bfloat16), "isl", scatter_dimension=2, tiled=True
    ).astype(jnp.float32)
    outer_delta = pseudo_sum / island_count
    new_momentum = nesterov_coef * momentum + outer_delta
    new_weights = weights - outer_rate * (outer_delta + nesterov_coef * new_momentum)
    return (new_weights, new_momentum)


def solution(mesh):
    in_specs = (
        P(None, "fsdp", "isl"),
        P(None, "fsdp", "isl"),
        P("isl", None, "fsdp", None),
        P("isl", None, "fsdp", None),
        P(None, ("isl", "fsdp"), None),
        P(None, ("isl", "fsdp"), None),
        P("isl", "fsdp"),
    )
    out_specs = (P(None, "fsdp", "isl"), P(None, "fsdp", "isl"))
    return jax.shard_map(body, mesh=mesh, in_specs=in_specs, out_specs=out_specs, check_vma=False)
```

profile of v0, /device:TPU:1, one launch (start us, length us, event | category | flops | bytes accessed | tf_op | source)
XLA Modules:
  0.0 474.0 jit_solution(12137875566399298339)
XLA Ops:
  10.6 96.8 %all_to_all.31 = bf16[4,3,224,1024]{3,2,1,0:T(8,128)(2,1)S(1)} all-to-all(bf16[4,3,224,1024]{3,2,1,0:T(8,128)(2,1)S(1)} %broadcast_in_dim.12), channel_id=1, replica_groups=mesh['isl'=4,'fsdp'=32] {'isl'}, dimensions={0} | all-to-all | bytes 11010048 | tf_op jit(solution)/shard_map/all_to_all | solution.py:26
  107.4 2.9 fusion.66
  114.6 3.1 copy.32
  123.0 26.2 %all-gather.2.cloned.1.call-done = bf16[2,256,4096]{2,1,0:T(8,128)(2,1)} async-done(((bf16[2,8,4096]{2,1,0:T(8,128)(2,1)}), bf16[2,256,4096]{2,1,0:T(8,128)(2,1)}) %all-gather.2.cloned.1.call-update) | async-done | bytes 4194320 | tf_op jit(solution)/shard_map/all_gather | solution.py:77
  149.2 3.1 fusion.34
  152.6 3.1 multiply_convert_fusion.5
  155.8 4.2 fusion.55
  160.0 6.8 %all-to-all-start.2 = ((f32[32,8,4096]{2,1,0:T(8,128)}), f32[32,8,4096]{2,1,0:T(8,128)}, u32[]{:S(2)}, u32[]{:S(2)}) async-start(f32[32,8,4096]{2,1,0:T(8,128)} %fusion.55), calls=%async_computation.2 | async-start | bytes 8388608 | tf_op jit(solution)/shard_map/all_to_all | solution.py:44
  167.5 34.9 %all-to-all-done.2 = f32[32,8,4096]{2,1,0:T(8,128)} async-done(((f32[32,8,4096]{2,1,0:T(8,128)}), f32[32,8,4096]{2,1,0:T(8,128)}, u32[]{:S(2)}, u32[]{:S(2)}) %all-to-all-start.2) | async-done | bytes 4194336 | tf_op jit(solution)/shard_map/all_to_all | solution.py:44
  203.0 9.3 %all-to-all-start.1 = ((s32[32,1,2]{2,1,0:T(1,128)}), s32[32,1,2]{2,1,0:T(1,128)S(1)}, u32[]{:S(2)}, u32[]{:S(2)}) async-start(s32[32,1,2]{2,1,0:T(1,128)} %broadcast_in_dim.13), calls=%async_computation.1 | async-start | bytes 32768 | tf_op jit(solution)/shard_map/all_to_all | solution.py:26
  212.3 2.4 reduce_sum.28
  214.8 5.1 %all-to-all-done.1 = s32[32,1,2]{2,1,0:T(1,128)S(1)} async-done(((s32[32,1,2]{2,1,0:T(1,128)}), s32[32,1,2]{2,1,0:T(1,128)S(1)}, u32[]{:S(2)}, u32[]{:S(2)}) %all-to-all-start.1) | async-done | bytes 288 | tf_op jit(solution)/shard_map/all_to_all | solution.py:26
  221.5 4.9 %all-to-all-start.3 = ((bf16[32,8,4096]{2,1,0:T(8,128)(2,1)}), bf16[32,8,4096]{2,1,0:T(8,128)(2,1)}, u32[]{:S(2)}, u32[]{:S(2)}) async-start(bf16[32,8,4096]{2,1,0:T(8,128)(2,1)} %broadcast_in_dim.14), calls=%async_computation.3 | async-start | bytes 4194304 | tf_op jit(solution)/shard_map/all_to_all | solution.py:26
  229.6 3.9 convert_bitcast_fusion
  233.6 6.5 %copy.39 = f32[4,3,28,8,1024]{4,3,0,2,1:T(8,128)} copy(f32[4,3,28,8,1024]{4,3,2,1,0:T(8,128)S(1)} %convert_bitcast_fusion) | data formatting | bytes 22020096 | tf_op jit(solution)/shard_map/convert_element_type | solution.py:67
  240.1 3.6 all-to-all-done.3
  243.7 2.5 fusion.16
  246.2 4.4 fusion.36
  252.3 2.5 slice-done.2
  256.1 11.3 %fusion.65 = bf16[3,224,4096]{2,1,0:T(8,128)(2,1)} fusion(f32[3,224,4096]{2,1,0:T(8,128)S(1)} %bitcast.142, bf16[1,3,224,4096]{3,2,1,0:T(8,128)(2,1)S(1)} %bitcast.148, f32[1,224,4096]{2,1,0:T(8,128)S(1)} %fusion.16, f32[1,224,4096]{2,1,0:T(8,128)S(1)} %fusion.17, f32[1,224,4096]{2,1,0:T(8,128)S(1)} %fusion.18, bf16[1,3,224,4096]{3,2,1,0:T(8,128)(2,1)} %param.9, ...), kind=kLoop, calls=%fused_computation.94 | loop fusion | flops 52297728 | bytes 38535168 | tf_op jit(solution)/shard_map/convert_element_type | solution.py:79
  269.8 2.4 multiply_convert_fusion.2
  274.5 32.4 %all_to_all.32 = f32[32,8,4096]{2,1,0:T(8,128)} all-to-all(f32[32,8,4096]{2,1,0:T(8,128)S(1)} %fusion.27), channel_id=1, replica_groups=mesh['isl'=4,'fsdp'=32] {'fsdp'}, dimensions={0} | all-to-all | bytes 8388608 | tf_op jit(solution)/shard_map/all_to_all | solution.py:44
  306.9 2.4 reduce_sum.29
  311.0 4.0 all-to-all-start.5
  315.8 26.2 %all-to-all-done.5 = bf16[32,8,4096]{2,1,0:T(8,128)(2,1)S(1)} async-done(((bf16[32,8,4096]{2,1,0:T(8,128)(2,1)}), bf16[32,8,4096]{2,1,0:T(8,128)(2,1)S(1)}, u32[]{:S(2)}, u32[]{:S(2)}) %all-to-all-start.5) | async-done | bytes 2097184 | tf_op jit(solution)/shard_map/all_to_all | solution.py:26
  342.1 2.4 fusion.43
  344.5 2.5 fusion.13
  347.1 5.0 %fusion.14 = f32[1,224,4096]{2,1,0:T(8,128)} fusion(bf16[2,256,4096]{2,1,0:T(8,128)(2,1)} %all-gather.2.cloned.1.call-done, f32[256,224]{0,1:T(8,128)S(1)} %fusion.43, f32[256,224]{0,1:T(8,128)S(1)} %fusion.40), kind=kOutput, calls=%fused_computation.27 | convolution fusion | flops 471023616 | bytes 6225920 | tf_op jit(solution)/shard_map/dot_general | solution.py:60
  352.0 2.5 fusion.15
  354.8 20.5 %fusion.12 = bf16[3,224,4096]{2,1,0:T(8,128)(2,1)} fusion(f32[3,224,4096]{2,1,0:T(8,128)S(1)} %bitcast.145, f32[1,224,4096]{2,1,0:T(8,128)} %fusion.13, f32[1,224,4096]{2,1,0:T(8,128)} %fusion.14, f32[1,224,4096]{2,1,0:T(8,128)S(1)} %fusion.15, f32[1,224,4096]{2,1,0:T(8,128)S(1)} %copy-done.4, f32[1,224,4096]{2,1,0:T(8,128)S(1)} %copy-done.6, ...), kind=kLoop, calls=%fused_computation.23 | loop fusion | flops 104595456 | bytes 49545216 | tf_op jit(solution)/shard_map/convert_element_type | solution.py:113
  375.4 86.1 %reduce-scatter.2.cloned.1.call-done = bf16[3,224,1024]{2,1,0:T(8,128)(2,1)} async-done(((bf16[3,224,4096]{2,1,0:T(8,128)(2,1)}), bf16[3,224,1024]{2,1,0:T(8,128)(2,1)}) %reduce-scatter.2.cloned.1.call-update) | async-done | bytes 1376272 | tf_op jit(solution)/shard_map/reduce_scatter | solution.py:112
  461.4 5.7 %multiply_subtract_fusion = (f32[3,224,1024]{2,1,0:T(8,128)}, f32[3,224,1024]{2,1,0:T(8,128)}) fusion(f32[3,224,1024]{2,1,0:T(8,128)S(1)} %copy-done.9, bf16[3,224,1024]{2,1,0:T(8,128)(2,1)} %reduce-scatter.2.cloned.1.call-done, f32[3,224,1024]{2,1,0:T(8,128)} %param.8), kind=kLoop, calls=%fused_computation.36 | loop fusion | flops 5505024 | bytes 12386304 | tf_op jit(solution)/shard_map/sub | solution.py:117
  (80 shorter events, 28.0 us)
Async XLA Ops:
  7.2 142.1 %all-gather.2.cloned.1.call-start = ((), (), s32[]{:S(2)}) async-start(), calls=%async_computation.7 | async-start | bytes 4325376 | tf_op jit(solution)/shard_map/all_gather | solution.py:77
  107.4 3.5 copy-start
  114.6 5.0 %copy-start.11 = (bf16[1,224,4,1024]{3,1,0,2:T(8,128)(2,1)S(1)}, bf16[1,224,4,1024]{3,1,0,2:T(8,128)(2,1)}, u32[]{:S(2)}) copy-start(bf16[1,224,4,1024]{3,1,0,2:T(8,128)(2,1)} %get-tuple-element.6) | copy-start | bytes 5505028
  149.2 3.4 copy-start.7
  155.7 4.3 copy-start.12
  160.0 42.4 %all-to-all-start.2 = ((f32[32,8,4096]{2,1,0:T(8,128)}), f32[32,8,4096]{2,1,0:T(8,128)}, u32[]{:S(2)}, u32[]{:S(2)}) async-start(f32[32,8,4096]{2,1,0:T(8,128)} %fusion.55), calls=%async_computation.2 | async-start | bytes 8388608 | tf_op jit(solution)/shard_map/all_to_all | solution.py:44
  166.8 48.0 %copy-start.13 = (bf16[2,8,4096]{2,1,0:T(8,128)(2,1)S(1)}, bf16[2,8,4096]{2,1,0:T(8,128)(2,1)}, u32[]{:S(2)}) copy-start(bf16[2,8,4096]{2,1,0:T(8,128)(2,1)} %param.11) | copy-start | bytes 393220
  166.8 47.9 %copy-start.16 = (bf16[2,8,4096]{2,1,0:T(8,128)(2,1)S(1)}, bf16[2,8,4096]{2,1,0:T(8,128)(2,1)}, u32[]{:S(2)}) copy-start(bf16[2,8,4096]{2,1,0:T(8,128)(2,1)} %param.12) | copy-start | bytes 393220
  203.0 16.9 %all-to-all-start.1 = ((s32[32,1,2]{2,1,0:T(1,128)}), s32[32,1,2]{2,1,0:T(1,128)S(1)}, u32[]{:S(2)}, u32[]{:S(2)}) async-start(s32[32,1,2]{2,1,0:T(1,128)} %broadcast_in_dim.13), calls=%async_computation.1 | async-start | bytes 32768 | tf_op jit(solution)/shard_map/all_to_all | solution.py:26
  221.5 22.2 %all-to-all-start.3 = ((bf16[32,8,4096]{2,1,0:T(8,128)(2,1)}), bf16[32,8,4096]{2,1,0:T(8,128)(2,1)}, u32[]{:S(2)}, u32[]{:S(2)}) async-start(bf16[32,8,4096]{2,1,0:T(8,128)(2,1)} %broadcast_in_dim.14), calls=%async_computation.3 | async-start | bytes 4194304 | tf_op jit(solution)/shard_map/all_to_all | solution.py:26
  233.5 12.6 %copy-start.10 = (bf16[28,8,4,1024]{3,1,2,0:T(8,128)(2,1)S(1)}, bf16[28,8,4,1024]{3,1,2,0:T(8,128)(2,1)}, u32[]{:S(2)}) copy-start(bf16[28,8,4,1024]{3,1,2,0:T(8,128)(2,1)} %copy.42) | copy-start | bytes 5505028
  243.7 7.0 %copy-start.8 = (bf16[2,256,4096]{2,1,0:T(8,128)(2,1)S(1)}, bf16[2,256,4096]{2,1,0:T(8,128)(2,1)}, u32[]{:S(2)}) copy-start(bf16[2,256,4096]{2,1,0:T(8,128)(2,1)} %all-gather.2.cloned.1.call-done) | copy-start | bytes 12582916
  243.7 8.4 %slice-start = ((s8[11010048]{0:T(1024)(128)(4,1)}), s8[4194304]{0:T(1024)(128)(4,1)S(1)}, s32[]{:S(2)}) async-start(s8[11010048]{0:T(1024)(128)(4,1)} %bitcast.140), calls=%async_computation.9 | async-start | bytes 8388608
  246.1 6.0 %copy-start.3 = (f32[1,224,4096]{2,1,0:T(8,128)}, f32[1,224,4096]{2,1,0:T(8,128)S(1)}, u32[]{:S(2)}) copy-start(f32[1,224,4096]{2,1,0:T(8,128)S(1)} %fusion.16) | copy-start | bytes 11010052
  246.1 5.2 %copy-start.15 = (f32[256,224]{0,1:T(8,128)S(1)}, f32[256,224]{0,1:T(8,128)}, u32[]{:S(2)}) copy-start(f32[256,224]{0,1:T(8,128)} %get-tuple-element.10) | copy-start | bytes 688132
  246.2 5.9 %slice-start.1 = ((s8[11010048]{0:T(1024)(128)(4,1)}), s8[4194304]{0:T(1024)(128)(4,1)S(1)}, s32[]{:S(2)}) async-start(s8[11010048]{0:T(1024)(128)(4,1)} %bitcast.140), calls=%async_computation.10 | async-start | bytes 8388608
  246.2 6.2 %slice-start.6 = ((s8[5505024]{0:T(1024)(128)(4,1)}), s8[4194304]{0:T(1024)(128)(4,1)S(1)}, s32[]{:S(2)}) async-start(s8[5505024]{0:T(1024)(128)(4,1)} %bitcast.147), calls=%async_computation.15 | async-start | bytes 8388608
  250.6 4.2 slice-start.2
  250.6 5.5 %slice-start.7 = ((s8[5505024]{0:T(1024)(128)(4,1)}), s8[1310720]{0:T(1024)(128)(4,1)S(1)}, s32[]{:S(2)}) async-start(s8[5505024]{0:T(1024)(128)(4,1)} %bitcast.147), calls=%async_computation.16 | async-start | bytes 2621440
  251.3 16.1 %copy-start.5 = (f32[1,224,4096]{2,1,0:T(8,128)}, f32[1,224,4096]{2,1,0:T(8,128)S(1)}, u32[]{:S(2)}) copy-start(f32[1,224,4096]{2,1,0:T(8,128)S(1)} %fusion.17) | copy-start | bytes 11010052
  252.1 15.3 %copy-start.1 = (f32[1,224,4096]{2,1,0:T(8,128)}, f32[1,224,4096]{2,1,0:T(8,128)S(1)}, u32[]{:S(2)}) copy-start(f32[1,224,4096]{2,1,0:T(8,128)S(1)} %fusion.18) | copy-start | bytes 11010052
  306.9 2.4 copy-start.14
  306.9 2.5 copy-start.17
  311.0 31.1 %all-to-all-start.5 = ((bf16[32,8,4096]{2,1,0:T(8,128)(2,1)}), bf16[32,8,4096]{2,1,0:T(8,128)(2,1)S(1)}, u32[]{:S(2)}, u32[]{:S(2)}) async-start(bf16[32,8,4096]{2,1,0:T(8,128)(2,1)} %broadcast_in_dim.15), calls=%async_computation.5 | async-start | bytes 4194304 | tf_op jit(solution)/shard_map/all_to_all | solution.py:26
  315.0 146.4 %reduce-scatter.2.cloned.1.call-start = ((), (), s32[]{:S(2)}) async-start(), calls=%async_computation.8 | async-start | bytes 6881280 | tf_op jit(solution)/shard_map/reduce_scatter | solution.py:112
  342.0 12.5 %slice-start.3 = ((s8[11010048]{0:T(1024)(128)(4,1)}), s8[4194304]{0:T(1024)(128)(4,1)S(1)}, s32[]{:S(2)}) async-start(s8[11010048]{0:T(1024)(128)(4,1)} %bitcast.143), calls=%async_computation.12 | async-start | bytes 8388608
  344.5 10.0 %slice-start.4 = ((s8[11010048]{0:T(1024)(128)(4,1)}), s8[4194304]{0:T(1024)(128)(4,1)S(1)}, s32[]{:S(2)}) async-start(s8[11010048]{0:T(1024)(128)(4,1)} %bitcast.143), calls=%async_computation.13 | async-start | bytes 8388608
  344.5 10.0 %copy-start.6 = (f32[1,224,4096]{2,1,0:T(8,128)S(1)}, f32[1,224,4096]{2,1,0:T(8,128)}, u32[]{:S(2)}) copy-start(f32[1,224,4096]{2,1,0:T(8,128)} %copy-done.5) | copy-start | bytes 11010052
  347.1 7.5 %slice-start.5 = ((s8[11010048]{0:T(1024)(128)(4,1)}), s8[2621440]{0:T(1024)(128)(4,1)S(1)}, s32[]{:S(2)}) async-start(s8[11010048]{0:T(1024)(128)(4,1)} %bitcast.143), calls=%async_computation.14 | async-start | bytes 5242880
  347.1 7.5 %copy-start.4 = (f32[1,224,4096]{2,1,0:T(8,128)S(1)}, f32[1,224,4096]{2,1,0:T(8,128)}, u32[]{:S(2)}) copy-start(f32[1,224,4096]{2,1,0:T(8,128)} %copy-done.3) | copy-start | bytes 11010052
  352.0 2.8 copy-start.2
  375.3 86.1 %copy-start.9 = (f32[3,224,1024]{2,1,0:T(8,128)S(1)}, f32[3,224,1024]{2,1,0:T(8,128)}, u32[]{:S(2)}) copy-start(f32[3,224,1024]{2,1,0:T(8,128)} %param.7) | copy-start | bytes 8257540
Sparse Core Ops, SparseCore 0:
  9.6 139.5 all-gather.1
  375.5 85.9 reduce-scatter.1
where the time goes:
time: 475 us; the launch traced here: 474 us
  waiting for transfers between devices  183 us (39%)
  blocking collectives  129 us (27%)
  other arithmetic  48.3 us (10%)
  matrix products  38.1 us (8%)
  local copies, waits for them, and re-layouts  33.9 us (7%)
  starting transfers between devices  25.4 us (5%)
  between operations  16.4 us (3%)
    all_to_all x1, blocking collectives, copy_for_each(): return lax.all_to_all(copies, axis, split_axis=0, concat_axis=0, tiled=True)  96.8 us
    reduce_scatter x1, waiting for transfers between devices, body(): lax.psum_scatter(pseudo_term.astype(jnp.bfloat16), 'isl', scatter_dimensi...  86.1 us
    all_to_all x3, waiting for transfers between devices, copy_for_each(): return lax.all_to_all(copies, axis, split_axis=0, concat_axis=0, tiled=True)  34.9 us
    all_to_all x1, waiting for transfers between devices, sum_at_owner(): lax.all_to_all(split_up(shard, dim, devices), axis, 0, 0, tiled=True)  34.9 us
    all_to_all x1, blocking collectives, sum_at_owner(): lax.all_to_all(split_up(shard, dim, devices), axis, 0, 0, tiled=True)  32.4 us
    all_gather x1, waiting for transfers between devices, body(): all_inputs = lax.all_gather(inputs, 'fsdp', axis=1, tiled=True)  26.2 us
    convert_element_type x1, other arithmetic, body(): pseudo_term.astype(jnp.bfloat16)  20.5 us
    all_to_all x3, starting transfers between devices, copy_for_each(): return lax.all_to_all(copies, axis, split_axis=0, concat_axis=0, tiled=True)  18.3 us
  transfers between devices with their start and end apart: 6, of which 6 were waited for; matrix products, arithmetic and copies ran while one was open for 7% of the time, Pallas kernels for 0%

commit v1 on v0

--- a/solution.py
+++ b/solution.py
@@ -74,7 +74,8 @@
         jnp.int32
     )
     overflow_counts = taken_together(overflow_marks, "fsdp")
-    all_inputs = lax.all_gather(inputs, "fsdp", axis=1, tiled=True)
+    stack = jnp.stack([inputs] * lax.axis_size("fsdp"))
+    all_inputs = jnp.concatenate(lax.all_to_all(stack, "fsdp", 0, 0), axis=1)
     for inner_step in range(inner_count):
         rounded = current.astype(jnp.bfloat16)
         local_inputs = inputs[inner_step]

time: 475 us -> 499 us (1.051)
  starting transfers between devices: 25.4 us -> 39.1 us
  waiting for transfers between devices: 183 us -> 195 us
  blocking collectives: 129 us -> 122 us
  matrix products: 38.1 us -> 43.4 us
    all_to_all x0 -> x1, waiting for transfers between devices: none -> 39.9 us  [body(): all_inputs = jnp.concatenate(lax.all_to_all(stack, 'fsdp', 0, 0), axis=1)]
    all_to_all x1, blocking collectives: 96.8 us -> 69.3 us  [copy_for_each(): return lax.all_to_all(copies, axis, split_axis=0, concat_axis=0, tiled=True)]
    all_gather x1 -> x0, waiting for transfers between devices: 26.2 us -> none  [body(): all_inputs = lax.all_gather(inputs, 'fsdp', axis=1, tiled=True)]
    reduce_scatter x1, waiting for transfers between devices: 86.1 us -> 63.1 us  [body(): lax.psum_scatter(pseudo_term.astype(jnp.bfloat16), 'isl', scatter_dimensi...]
    all_to_all x1, blocking collectives: 32.4 us -> 52.3 us  [sum_at_owner(): lax.all_to_all(split_up(shard, dim, devices), axis, 0, 0, tiled=True)]
    all_to_all x1, waiting for transfers between devices: 34.9 us -> 50.4 us  [sum_at_owner(): lax.all_to_all(split_up(shard, dim, devices), axis, 0, 0, tiled=True)]
    all_to_all x0 -> x1, starting transfers between devices: none -> 7.62 us  [body(): all_inputs = jnp.concatenate(lax.all_to_all(stack, 'fsdp', 0, 0), axis=1)]
    all_to_all x3, waiting for transfers between devices: 34.9 us -> 41.5 us  [copy_for_each(): return lax.all_to_all(copies, axis, split_axis=0, concat_axis=0, tiled=True)]
where the time goes in v1:
time: 499 us; the launch traced here: 498 us
  waiting for transfers between devices  195 us (39%)
  blocking collectives  122 us (24%)
  other arithmetic  48.1 us (10%)
  matrix products  43.4 us (9%)
  starting transfers between devices  39.1 us (8%)
  local copies, waits for them, and re-layouts  34.1 us (7%)
  between operations  16.5 us (3%)
    all_to_all x1, blocking collectives, copy_for_each(): return lax.all_to_all(copies, axis, split_axis=0, concat_axis=0, tiled=True)  69.3 us
    reduce_scatter x1, waiting for transfers between devices, body(): lax.psum_scatter(pseudo_term.astype(jnp.bfloat16), 'isl', scatter_dimensi...  63.1 us
    all_to_all x1, blocking collectives, sum_at_owner(): lax.all_to_all(split_up(shard, dim, devices), axis, 0, 0, tiled=True)  52.3 us
    all_to_all x1, waiting for transfers between devices, sum_at_owner(): lax.all_to_all(split_up(shard, dim, devices), axis, 0, 0, tiled=True)  50.4 us
    all_to_all x3, waiting for transfers between devices, copy_for_each(): return lax.all_to_all(copies, axis, split_axis=0, concat_axis=0, tiled=True)  41.5 us
    all_to_all x1, waiting for transfers between devices, body(): all_inputs = jnp.concatenate(lax.all_to_all(stack, 'fsdp', 0, 0), axis=1)  39.9 us
    all_to_all x3, starting transfers between devices, copy_for_each(): return lax.all_to_all(copies, axis, split_axis=0, concat_axis=0, tiled=True)  23.7 us
    convert_element_type x1, other arithmetic, body(): pseudo_term.astype(jnp.bfloat16)  20.4 us
  transfers between devices with their start and end apart: 6, of which 6 were waited for; matrix products, arithmetic and copies ran while one was open for 7% of the time, Pallas kernels for 0%

profile of v1, /device:TPU:1, one launch (start us, length us, event | category | flops | bytes accessed | tf_op | source)
XLA Modules:
  0.0 497.7 jit_solution(10932192148129667895)
XLA Ops:
  9.9 69.3 %all_to_all.36 = bf16[4,3,224,1024]{3,2,1,0:T(8,128)(2,1)} all-to-all(bf16[4,3,224,1024]{3,2,1,0:T(8,128)(2,1)S(1)} %broadcast_in_dim.12), channel_id=1, replica_groups=mesh['isl'=4,'fsdp'=32] {'isl'}, dimensions={0} | all-to-all | bytes 11010048 | tf_op jit(solution)/shard_map/all_to_all | solution.py:26
  79.2 2.5 stack.18
  81.8 7.6 %all-to-all-start.2 = ((bf16[32,2,8,4096]{3,2,1,0:T(8,128)(2,1)}), bf16[32,2,8,4096]{3,2,1,0:T(8,128)(2,1)}, u32[]{:S(2)}, u32[]{:S(2)}) async-start(bf16[32,2,8,4096]{3,2,1,0:T(8,128)(2,1)} %stack.18), calls=%async_computation.2 | async-start | bytes 8388608 | tf_op jit(solution)/shard_map/all_to_all | solution.py:78
  89.4 5.1 %fusion.66 = (bf16[1,224,4,1024]{3,1,0,2:T(8,128)(2,1)S(1)}, bf16[1,224,4,1024]{3,1,0,2:T(8,128)(2,1)}, bf16[1,224,4,1024]{3,1,0,2:T(8,128)(2,1)}) fusion(bf16[3,224,4,1024]{3,1,0,2:T(8,128)(2,1)} %bitcast.147), kind=kLoop, calls=%fused_computation.95 | loop fusion | bytes 11010048 | tf_op jit(solution)/shard_map/slice | solution.py:88
  98.2 3.1 copy.32
  106.6 39.9 %all-to-all-done.2 = bf16[32,2,8,4096]{3,2,1,0:T(8,128)(2,1)} async-done(((bf16[32,2,8,4096]{3,2,1,0:T(8,128)(2,1)}), bf16[32,2,8,4096]{3,2,1,0:T(8,128)(2,1)}, u32[]{:S(2)}, u32[]{:S(2)}) %all-to-all-start.2) | async-done | bytes 4194336 | tf_op jit(solution)/shard_map/all_to_all | solution.py:78
  146.5 3.1 fusion.34
  149.6 3.1 multiply_convert_fusion.5
  152.8 4.2 fusion.55
  157.0 7.7 %all-to-all-start.3 = ((f32[32,8,4096]{2,1,0:T(8,128)}), f32[32,8,4096]{2,1,0:T(8,128)}, u32[]{:S(2)}, u32[]{:S(2)}) async-start(f32[32,8,4096]{2,1,0:T(8,128)} %fusion.55), calls=%async_computation.3 | async-start | bytes 8388608 | tf_op jit(solution)/shard_map/all_to_all | solution.py:44
  165.4 50.4 %all-to-all-done.3 = f32[32,8,4096]{2,1,0:T(8,128)} async-done(((f32[32,8,4096]{2,1,0:T(8,128)}), f32[32,8,4096]{2,1,0:T(8,128)}, u32[]{:S(2)}, u32[]{:S(2)}) %all-to-all-start.3) | async-done | bytes 4194336 | tf_op jit(solution)/shard_map/all_to_all | solution.py:44
  216.4 10.2 %all-to-all-start.1 = ((s32[32,1,2]{2,1,0:T(1,128)}), s32[32,1,2]{2,1,0:T(1,128)S(1)}, u32[]{:S(2)}, u32[]{:S(2)}) async-start(s32[32,1,2]{2,1,0:T(1,128)} %broadcast_in_dim.13), calls=%async_computation.1 | async-start | bytes 32768 | tf_op jit(solution)/shard_map/all_to_all | solution.py:26
  229.1 4.6 all-to-all-done.1
  235.3 4.8 all-to-all-start.4
  243.4 3.9 convert_bitcast_fusion
  247.3 6.5 %copy.39 = f32[4,3,28,8,1024]{4,3,0,2,1:T(8,128)} copy(f32[4,3,28,8,1024]{4,3,2,1,0:T(8,128)S(1)} %convert_bitcast_fusion) | data formatting | bytes 22020096 | tf_op jit(solution)/shard_map/convert_element_type | solution.py:67
  253.8 10.7 %all-to-all-done.4 = bf16[32,8,4096]{2,1,0:T(8,128)(2,1)} async-done(((bf16[32,8,4096]{2,1,0:T(8,128)(2,1)}), bf16[32,8,4096]{2,1,0:T(8,128)(2,1)}, u32[]{:S(2)}, u32[]{:S(2)}) %all-to-all-start.4) | async-done | bytes 2097184 | tf_op jit(solution)/shard_map/all_to_all | solution.py:26
  264.5 2.5 fusion.36
  269.6 4.2 fusion.18
  273.8 3.6 fusion.16
  277.5 11.2 %fusion.65 = bf16[3,224,4096]{2,1,0:T(8,128)(2,1)S(1)} fusion(f32[3,224,4096]{2,1,0:T(8,128)S(1)} %bitcast.143, bf16[1,3,224,4096]{3,2,1,0:T(8,128)(2,1)S(1)} %bitcast.149, f32[1,224,4096]{2,1,0:T(8,128)S(1)} %fusion.16, f32[1,224,4096]{2,1,0:T(8,128)S(1)} %fusion.17, f32[1,224,4096]{2,1,0:T(8,128)S(1)} %fusion.18, bf16[1,3,224,4096]{3,2,1,0:T(8,128)(2,1)} %param.9, ...), kind=kLoop, calls=%fused_computation.94 | loop fusion | flops 52297728 | bytes 38535168 | tf_op jit(solution)/shard_map/convert_element_type | solution.py:80
  288.7 4.0 fusion.40
  297.4 52.3 %all_to_all.37 = f32[32,8,4096]{2,1,0:T(8,128)} all-to-all(f32[32,8,4096]{2,1,0:T(8,128)S(1)} %fusion.27), channel_id=1, replica_groups=mesh['isl'=4,'fsdp'=32] {'fsdp'}, dimensions={0} | all-to-all | bytes 8388608 | tf_op jit(solution)/shard_map/all_to_all | solution.py:44
  349.7 2.4 reduce_sum.29
  353.8 8.7 %all-to-all-start.6 = ((bf16[32,8,4096]{2,1,0:T(8,128)(2,1)}), bf16[32,8,4096]{2,1,0:T(8,128)(2,1)S(1)}, u32[]{:S(2)}, u32[]{:S(2)}) async-start(bf16[32,8,4096]{2,1,0:T(8,128)(2,1)} %broadcast_in_dim.15), calls=%async_computation.6 | async-start | bytes 4194304 | tf_op jit(solution)/shard_map/all_to_all | solution.py:26
  363.2 26.1 %all-to-all-done.6 = bf16[32,8,4096]{2,1,0:T(8,128)(2,1)S(1)} async-done(((bf16[32,8,4096]{2,1,0:T(8,128)(2,1)}), bf16[32,8,4096]{2,1,0:T(8,128)(2,1)S(1)}, u32[]{:S(2)}, u32[]{:S(2)}) %all-to-all-start.6) | async-done | bytes 2097184 | tf_op jit(solution)/shard_map/all_to_all | solution.py:26
  391.8 4.2 fusion.14
  396.0 2.5 fusion.15
  398.5 2.6 fusion.13
  401.6 20.4 %fusion.12 = bf16[3,224,4096]{2,1,0:T(8,128)(2,1)} fusion(f32[3,224,4096]{2,1,0:T(8,128)S(1)} %bitcast.146, f32[1,224,4096]{2,1,0:T(8,128)} %fusion.13, f32[1,224,4096]{2,1,0:T(8,128)} %fusion.14, f32[1,224,4096]{2,1,0:T(8,128)S(1)} %fusion.15, f32[1,224,4096]{2,1,0:T(8,128)S(1)} %copy-done.5, f32[1,224,4096]{2,1,0:T(8,128)S(1)} %copy-done.3, ...), kind=kLoop, calls=%fused_computation.23 | loop fusion | flops 104595456 | bytes 49545216 | tf_op jit(solution)/shard_map/convert_element_type | solution.py:114
  422.0 63.1 %reduce-scatter.2.cloned.1.call-done = bf16[3,224,1024]{2,1,0:T(8,128)(2,1)} async-done(((bf16[3,224,4096]{2,1,0:T(8,128)(2,1)}), bf16[3,224,1024]{2,1,0:T(8,128)(2,1)}) %reduce-scatter.2.cloned.1.call-update) | async-done | bytes 1376272 | tf_op jit(solution)/shard_map/reduce_scatter | solution.py:113
  485.2 5.7 %multiply_subtract_fusion = (f32[3,224,1024]{2,1,0:T(8,128)}, f32[3,224,1024]{2,1,0:T(8,128)}) fusion(f32[3,224,1024]{2,1,0:T(8,128)S(1)} %copy-done.6, bf16[3,224,1024]{2,1,0:T(8,128)(2,1)} %reduce-scatter.2.cloned.1.call-done, f32[3,224,1024]{2,1,0:T(8,128)} %param.8), kind=kLoop, calls=%fused_computation.36 | loop fusion | flops 5505024 | bytes 12386304 | tf_op jit(solution)/shard_map/sub | solution.py:118
  (80 shorter events, 31.0 us)
Async XLA Ops:
  9.9 69.3 %copy-start.13 = (bf16[2,8,4096]{2,1,0:T(8,128)(2,1)S(1)}, bf16[2,8,4096]{2,1,0:T(8,128)(2,1)}, u32[]{:S(2)}) copy-start(bf16[2,8,4096]{2,1,0:T(8,128)(2,1)} %param.11) | copy-start | bytes 393220
  81.8 64.7 %all-to-all-start.2 = ((bf16[32,2,8,4096]{3,2,1,0:T(8,128)(2,1)}), bf16[32,2,8,4096]{3,2,1,0:T(8,128)(2,1)}, u32[]{:S(2)}, u32[]{:S(2)}) async-start(bf16[32,2,8,4096]{3,2,1,0:T(8,128)(2,1)} %stack.18), calls=%async_computation.2 | async-start | bytes 8388608 | tf_op jit(solution)/shard_map/all_to_all | solution.py:78
  98.2 5.1 %copy-start.9 = (bf16[1,224,4,1024]{3,1,0,2:T(8,128)(2,1)S(1)}, bf16[1,224,4,1024]{3,1,0,2:T(8,128)(2,1)}, u32[]{:S(2)}) copy-start(bf16[1,224,4,1024]{3,1,0,2:T(8,128)(2,1)} %get-tuple-element.6) | copy-start | bytes 5505028
  146.5 3.1 copy-start.10
  152.7 4.3 copy-start.11
  157.0 58.8 %all-to-all-start.3 = ((f32[32,8,4096]{2,1,0:T(8,128)}), f32[32,8,4096]{2,1,0:T(8,128)}, u32[]{:S(2)}, u32[]{:S(2)}) async-start(f32[32,8,4096]{2,1,0:T(8,128)} %fusion.55), calls=%async_computation.3 | async-start | bytes 8388608 | tf_op jit(solution)/shard_map/all_to_all | solution.py:44
  164.7 64.4 %copy-start.16 = (bf16[2,8,4096]{2,1,0:T(8,128)(2,1)S(1)}, bf16[2,8,4096]{2,1,0:T(8,128)(2,1)}, u32[]{:S(2)}) copy-start(bf16[2,8,4096]{2,1,0:T(8,128)(2,1)} %param.12) | copy-start | bytes 393220
  216.4 17.3 %all-to-all-start.1 = ((s32[32,1,2]{2,1,0:T(1,128)}), s32[32,1,2]{2,1,0:T(1,128)S(1)}, u32[]{:S(2)}, u32[]{:S(2)}) async-start(s32[32,1,2]{2,1,0:T(1,128)} %broadcast_in_dim.13), calls=%async_computation.1 | async-start | bytes 32768 | tf_op jit(solution)/shard_map/all_to_all | solution.py:26
  235.3 29.2 %all-to-all-start.4 = ((bf16[32,8,4096]{2,1,0:T(8,128)(2,1)}), bf16[32,8,4096]{2,1,0:T(8,128)(2,1)}, u32[]{:S(2)}, u32[]{:S(2)}) async-start(bf16[32,8,4096]{2,1,0:T(8,128)(2,1)} %broadcast_in_dim.14), calls=%async_computation.4 | async-start | bytes 4194304 | tf_op jit(solution)/shard_map/all_to_all | solution.py:26
  247.3 17.3 %copy-start.8 = (bf16[28,8,4,1024]{3,1,2,0:T(8,128)(2,1)S(1)}, bf16[28,8,4,1024]{3,1,2,0:T(8,128)(2,1)}, u32[]{:S(2)}) copy-start(bf16[28,8,4,1024]{3,1,2,0:T(8,128)(2,1)} %copy.42) | copy-start | bytes 5505028
  264.5 5.0 %copy-start.15 = (f32[256,224]{0,1:T(8,128)S(1)}, f32[256,224]{0,1:T(8,128)}, u32[]{:S(2)}) copy-start(f32[256,224]{0,1:T(8,128)} %get-tuple-element.10) | copy-start | bytes 688132
  264.5 12.9 %slice-start = ((s8[11010048]{0:T(1024)(128)(4,1)}), s8[4194304]{0:T(1024)(128)(4,1)S(1)}, s32[]{:S(2)}) async-start(s8[11010048]{0:T(1024)(128)(4,1)} %bitcast.141), calls=%async_computation.9 | async-start | bytes 8388608
  267.1 10.4 %slice-start.1 = ((s8[11010048]{0:T(1024)(128)(4,1)}), s8[4194304]{0:T(1024)(128)(4,1)S(1)}, s32[]{:S(2)}) async-start(s8[11010048]{0:T(1024)(128)(4,1)} %bitcast.141), calls=%async_computation.10 | async-start | bytes 8388608
  267.1 10.4 %slice-start.6 = ((s8[5505024]{0:T(1024)(128)(4,1)}), s8[4194304]{0:T(1024)(128)(4,1)S(1)}, s32[]{:S(2)}) async-start(s8[5505024]{0:T(1024)(128)(4,1)} %bitcast.148), calls=%async_computation.15 | async-start | bytes 8388608
  269.5 7.9 %copy-start.2 = (f32[1,224,4096]{2,1,0:T(8,128)}, f32[1,224,4096]{2,1,0:T(8,128)S(1)}, u32[]{:S(2)}) copy-start(f32[1,224,4096]{2,1,0:T(8,128)S(1)} %fusion.17) | copy-start | bytes 11010052
  269.6 4.2 copy-start.12
  269.6 7.9 %slice-start.2 = ((s8[11010048]{0:T(1024)(128)(4,1)}), s8[2621440]{0:T(1024)(128)(4,1)S(1)}, s32[]{:S(2)}) async-start(s8[11010048]{0:T(1024)(128)(4,1)} %bitcast.141), calls=%async_computation.11 | async-start | bytes 5242880
  269.6 7.9 %slice-start.7 = ((s8[5505024]{0:T(1024)(128)(4,1)}), s8[1310720]{0:T(1024)(128)(4,1)S(1)}, s32[]{:S(2)}) async-start(s8[5505024]{0:T(1024)(128)(4,1)} %bitcast.148), calls=%async_computation.16 | async-start | bytes 2621440
  273.8 14.9 %copy-start = (f32[1,224,4096]{2,1,0:T(8,128)}, f32[1,224,4096]{2,1,0:T(8,128)S(1)}, u32[]{:S(2)}) copy-start(f32[1,224,4096]{2,1,0:T(8,128)S(1)} %fusion.18) | copy-start | bytes 11010052
  277.4 11.3 %copy-start.4 = (f32[1,224,4096]{2,1,0:T(8,128)}, f32[1,224,4096]{2,1,0:T(8,128)S(1)}, u32[]{:S(2)}) copy-start(f32[1,224,4096]{2,1,0:T(8,128)S(1)} %fusion.16) | copy-start | bytes 11010052
  288.7 6.4 %copy-start.7 = (bf16[3,224,4096]{2,1,0:T(8,128)(2,1)}, bf16[3,224,4096]{2,1,0:T(8,128)(2,1)S(1)}, u32[]{:S(2)}) copy-start(bf16[3,224,4096]{2,1,0:T(8,128)(2,1)S(1)} %fusion.65) | copy-start | bytes 16515076
  349.7 2.4 copy-start.14
  349.7 2.5 copy-start.17
  353.8 35.5 %all-to-all-start.6 = ((bf16[32,8,4096]{2,1,0:T(8,128)(2,1)}), bf16[32,8,4096]{2,1,0:T(8,128)(2,1)S(1)}, u32[]{:S(2)}, u32[]{:S(2)}) async-start(bf16[32,8,4096]{2,1,0:T(8,128)(2,1)} %broadcast_in_dim.15), calls=%async_computation.6 | async-start | bytes 4194304 | tf_op jit(solution)/shard_map/all_to_all | solution.py:26
  362.5 122.7 %reduce-scatter.2.cloned.1.call-start = ((), (), s32[]{:S(2)}) async-start(), calls=%async_computation.8 | async-start | bytes 6881280 | tf_op jit(solution)/shard_map/reduce_scatter | solution.py:113
  389.3 11.7 %slice-start.3 = ((s8[11010048]{0:T(1024)(128)(4,1)}), s8[4194304]{0:T(1024)(128)(4,1)S(1)}, s32[]{:S(2)}) async-start(s8[11010048]{0:T(1024)(128)(4,1)} %bitcast.144), calls=%async_computation.12 | async-start | bytes 8388608
  391.7 9.3 %slice-start.4 = ((s8[11010048]{0:T(1024)(128)(4,1)}), s8[4194304]{0:T(1024)(128)(4,1)S(1)}, s32[]{:S(2)}) async-start(s8[11010048]{0:T(1024)(128)(4,1)} %bitcast.144), calls=%async_computation.13 | async-start | bytes 8388608
  391.8 9.3 %copy-start.5 = (f32[1,224,4096]{2,1,0:T(8,128)S(1)}, f32[1,224,4096]{2,1,0:T(8,128)}, u32[]{:S(2)}) copy-start(f32[1,224,4096]{2,1,0:T(8,128)} %copy-done.4) | copy-start | bytes 11010052
  396.0 5.1 %slice-start.5 = ((s8[11010048]{0:T(1024)(128)(4,1)}), s8[2621440]{0:T(1024)(128)(4,1)S(1)}, s32[]{:S(2)}) async-start(s8[11010048]{0:T(1024)(128)(4,1)} %bitcast.144), calls=%async_computation.14 | async-start | bytes 5242880
  396.0 5.1 %copy-start.3 = (f32[1,224,4096]{2,1,0:T(8,128)S(1)}, f32[1,224,4096]{2,1,0:T(8,128)}, u32[]{:S(2)}) copy-start(f32[1,224,4096]{2,1,0:T(8,128)} %copy-done.2) | copy-start | bytes 11010052
  398.5 3.1 copy-start.1
  422.0 63.2 %copy-start.6 = (f32[3,224,1024]{2,1,0:T(8,128)S(1)}, f32[3,224,1024]{2,1,0:T(8,128)}, u32[]{:S(2)}) copy-start(f32[3,224,1024]{2,1,0:T(8,128)} %param.7) | copy-start | bytes 8257540
Sparse Core Ops, SparseCore 0:
  422.1 62.9 reduce-scatter.1
